TPU v7x, 32 devices: a whole 2x2x4 slice. The times are simulated.
32 devices in a mesh: rep: 8 (over z, core), tp: 4 (over y, x).
Axes of the slice: x: 2, y: 2, z: 4, core: 2. Of those that a mesh axis runs over, the one named last changes fastest.
Arguments:
- hidden: bfloat16 [32, 4608], P('rep'), may hold values from -6 to 6
- positions: int32 [32], P('rep'), may hold values from 1 to 1023
- key_cache: bfloat16 [32, 16, 1024, 128], P('rep', 'tp'), may hold values from -6 to 6
- value_cache: bfloat16 [32, 16, 1024, 128], P('rep', 'tp'), may hold values from -6 to 6
- norm_gain: float32 [4608], replicated, may hold values from 0.1 to 1.9
- q_proj: bfloat16 [4096, 4608], P(('rep', 'tp')), may hold values from -0.09375 to 0.09375
- k_proj: bfloat16 [2048, 4608], P(('rep', 'tp')), may hold values from -0.09375 to 0.09375
- v_proj: bfloat16 [2048, 4608], P(('rep', 'tp')), may hold values from -0.09375 to 0.09375
- o_proj: bfloat16 [4608, 4096], P(('rep', 'tp')), may hold values from -0.09375 to 0.09375
- post_gain: float32 [4608], P('tp'), may hold values from 0.1 to 1.9
Outputs:
- joined_qkv: bfloat16 [4608, 8192], P(None, 'tp')
- wo_heads: bfloat16 [4096, 4608], P('tp')
- attn_out: bfloat16 [32, 4608], P('rep', 'tp')
All inputs are finite; a program needn't handle non-finite values.
Results may differ from a plain program's by a relative error of at most 0.008.
Values may be sent and summed in bfloat16 or wider, within the bound.
A program may use at most 128 MiB of HBM per device.

v0:
```python
import jax
import jax.numpy as jnp
from jax import lax
from jax.sharding import PartitionSpec as P

score_scale = 144.0 ** (-0.5)
soft_cap = 50.0


def rms_scale(values, gain):
    mean_square = jnp.mean(values * values, axis=-1, keepdims=True)
    return values * lax.rsqrt(mean_square + 1e-06) * gain


def rotate(values, positions):
    half = values.shape[-1] // 2
    freq = 10000.0 ** (-2.0 * jnp.arange(half, dtype=jnp.float32) / values.shape[-1])
    angle = positions.astype(jnp.float32)[:, None] * freq[None, :]
    cosine = jnp.cos(angle)[:, None, :]
    sine = jnp.sin(angle)[:, None, :]
    first = values[..., :half]
    second = values[..., half:]
    return jnp.concatenate(
        [first * cosine - second * sine, second * cosine + first * sine], axis=-1
    )


def body(
    hidden, positions, key_cache, value_cache, norm_gain, q_proj, k_proj, v_proj, o_proj, post_gain
):
    tp_count = lax.axis_size("tp")
    replica_count = lax.axis_size("rep")
    per_tp = replica_count // tp_count
    model_width = hidden.shape[1]
    stacked = (
        lax.all_gather(q_proj[None], "rep", axis=0, tiled=True),
        lax.all_gather(k_proj[None], "rep", axis=0, tiled=True),
        lax.all_gather(v_proj[None], "rep", axis=0, tiled=True),
    )
    shaped = [matrix.reshape((tp_count, per_tp, 1) + matrix.shape[1:]) for matrix in stacked]
    arrived = (
        lax.all_to_all(shaped[0], "tp", split_axis=0, concat_axis=2, tiled=True),
        lax.all_to_all(shaped[1], "tp", split_axis=0, concat_axis=2, tiled=True),
        lax.all_to_all(shaped[2], "tp", split_axis=0, concat_axis=2, tiled=True),
    )
    head_block = [matrix.reshape(-1, model_width) for matrix in arrived]
    joined_block = jnp.transpose(jnp.concatenate(head_block, axis=0))
    split_cols = o_proj.reshape(o_proj.shape[0], tp_count, -1)
    rows_of_group = lax.all_to_all(split_cols, "tp", split_axis=1, concat_axis=0, tiled=True)
    complete_rows = lax.all_gather(rows_of_group, "rep", axis=0, tiled=True)
    out_block = jnp.transpose(complete_rows.reshape(model_width, -1))
    batch, kv_local, length, head_dim = key_cache.shape
    q_width = head_block[0].shape[0]
    kv_width = head_block[1].shape[0]
    q_local = q_width // head_dim
    group = q_local // kv_local
    normed = rms_scale(hidden.astype(jnp.float32), norm_gain).astype(jnp.bfloat16)
    query_key_value_projected = jnp.dot(normed, joined_block, preferred_element_type=jnp.float32)
    query = query_key_value_projected[:, :q_width].reshape(batch, q_local, head_dim)
    keys_new = query_key_value_projected[:, q_width : q_width + kv_width].reshape(
        batch, kv_local, head_dim
    )
    values_new = query_key_value_projected[:, q_width + kv_width :].reshape(
        batch, kv_local, head_dim
    )
    query_rot = rotate(query, positions).astype(jnp.bfloat16)
    rotated_keys = rotate(keys_new, positions).astype(jnp.bfloat16)
    values_rot = values_new.astype(jnp.bfloat16)
    grouped_heads = query_rot.reshape(batch, kv_local, group, head_dim)
    scores = (
        jnp.einsum("bkgd,bkld->bkgl", grouped_heads, key_cache, preferred_element_type=jnp.float32)
        * score_scale
    )
    capped = soft_cap * jnp.tanh(scores / soft_cap)
    valid = jnp.arange(length, dtype=jnp.int32)[None, :] < positions[:, None]
    weight_raw = jnp.where(valid[:, None, None, :], jnp.exp(capped), 0.0)
    self_score = (
        jnp.einsum("juzy,juy->juz", grouped_heads, rotated_keys, preferred_element_type=jnp.float32)
        * score_scale
    )
    self_raw = jnp.exp(soft_cap * jnp.tanh(self_score / soft_cap))
    denom = jnp.sum(weight_raw, axis=-1) + self_raw
    weights = (weight_raw / denom[..., None]).astype(jnp.bfloat16)
    self_weight = (self_raw / denom).astype(jnp.bfloat16)
    attention = jnp.einsum(
        "bkgl,bkld->bkgd", weights, value_cache, preferred_element_type=jnp.float32
    )
    attention = (
        attention
        + self_weight.astype(jnp.float32)[..., None] * values_rot.astype(jnp.float32)[:, :, None, :]
    )
    attention = attention.reshape(batch, q_width).astype(jnp.bfloat16)
    partial_out = jnp.dot(attention, out_block, preferred_element_type=jnp.float32)
    width_local = post_gain.shape[0]
    total = lax.psum(partial_out, "tp")
    multiplier = lax.rsqrt(jnp.mean(total * total, axis=1) + 1e-06)
    share = lax.dynamic_slice_in_dim(total, lax.axis_index("tp") * width_local, width_local, 1)
    result = share * multiplier[:, None] * post_gain
    return (joined_block, out_block, result.astype(jnp.bfloat16))


def solution(mesh):
    in_specs = (
        P("rep", None),
        P("rep"),
        P("rep", "tp", None, None),
        P("rep", "tp", None, None),
        P(),
        P(("rep", "tp"), None),
        P(("rep", "tp"), None),
        P(("rep", "tp"), None),
        P(("rep", "tp"), None),
        P("tp"),
    )
    out_specs = (P(None, "tp"), P("tp", None), P("rep", "tp"))
    return jax.shard_map(body, mesh=mesh, in_specs=in_specs, out_specs=out_specs, check_vma=False)
```

profile of v0, /device:TPU:0, one launch (start us, length us, event | category | flops | bytes accessed | tf_op | source)
XLA Modules:
  0.0 437.0 jit_solution(3041150683269415164)
XLA Ops:
  7.2 0.7 all-gather.14.cloned.1.call-update
  7.9 0.7 all-gather.12.cloned.1.call-update
  8.7 0.7 all-gather.10.cloned.1.call-update
  9.4 1.4 copy.53
  10.8 20.6 %all_to_all.63 = bf16[144,4,1024]{2,0,1:T(8,128)(2,1)} all-to-all(bf16[144,4,1024]{2,0,1:T(8,128)(2,1)S(1)} %bitcast.63), channel_id=1, replica_groups=mesh['rep'=8,'tp'=4] {'tp'}, dimensions={1} | all-to-all | bytes 2359296 | tf_op jit(solution)/shard_map/all_to_all | solution.py:49
  31.5 32.1 %all-gather.14.cloned.1.call-done = bf16[512,4608]{1,0:T(8,128)(2,1)} async-done(((bf16[64,4608]{1,0:T(8,128)(2,1)}), bf16[512,4608]{1,0:T(8,128)(2,1)}) %all-gather.14.cloned.1.call-update) | async-done | bytes 4718608 | tf_op jit(solution)/shard_map/all_gather | solution.py:38
  63.6 5.0 %all-to-all-start.2 = ((bf16[4,2,1,64,4608]{4,3,1,2,0:T(8,128)(2,1)}), bf16[4,2,1,64,4608]{4,3,1,2,0:T(8,128)(2,1)}, u32[]{:S(2)}, u32[]{:S(2)}) async-start(bf16[4,2,1,64,4608]{4,3,1,2,0:T(8,128)(2,1)} %bitcast.61), calls=%async_computation.2 | async-start | bytes 9437184 | tf_op jit(solution)/shard_map/all_to_all | solution.py:44
  68.5 46.7 %all-gather.12.cloned.1.call-done = bf16[512,4608]{1,0:T(8,128)(2,1)} async-done(((bf16[64,4608]{1,0:T(8,128)(2,1)}), bf16[512,4608]{1,0:T(8,128)(2,1)}) %all-gather.12.cloned.1.call-update) | async-done | bytes 4718608 | tf_op jit(solution)/shard_map/all_gather | solution.py:37
  115.2 7.0 %all-to-all-done.2 = bf16[4,2,1,64,4608]{4,3,1,2,0:T(8,128)(2,1)} async-done(((bf16[4,2,1,64,4608]{4,3,1,2,0:T(8,128)(2,1)}), bf16[4,2,1,64,4608]{4,3,1,2,0:T(8,128)(2,1)}, u32[]{:S(2)}, u32[]{:S(2)}) %all-to-all-start.2) | async-done | bytes 4718624 | tf_op jit(solution)/shard_map/all_to_all | solution.py:44
  122.2 5.0 %all-to-all-start.1 = ((bf16[4,2,1,64,4608]{4,3,1,2,0:T(8,128)(2,1)}), bf16[4,2,1,64,4608]{4,3,1,2,0:T(8,128)(2,1)}, u32[]{:S(2)}, u32[]{:S(2)}) async-start(bf16[4,2,1,64,4608]{4,3,1,2,0:T(8,128)(2,1)} %bitcast.60), calls=%async_computation.1 | async-start | bytes 9437184 | tf_op jit(solution)/shard_map/all_to_all | solution.py:43
  127.3 79.1 %all-gather.10.cloned.1.call-done = bf16[1024,4608]{1,0:T(8,128)(2,1)} async-done(((bf16[128,4608]{1,0:T(8,128)(2,1)}), bf16[1024,4608]{1,0:T(8,128)(2,1)}) %all-gather.10.cloned.1.call-update) | async-done | bytes 9437200 | tf_op jit(solution)/shard_map/all_gather | solution.py:36
  206.4 23.7 %copy.36 = bf16[4,2,1,128,4608]{3,1,4,2,0:T(2,128)(2,1)} copy(bf16[4,2,1,128,4608]{4,3,1,0,2:T(8,128)(2,1)} %bitcast.59) | data formatting | bytes 18874368 | tf_op jit(solution)/shard_map/reshape | solution.py:40
  230.1 6.0 %all-to-all-start = ((bf16[4,2,1,128,4608]{3,1,4,2,0:T(2,128)(2,1)}), bf16[4,2,1,128,4608]{3,1,4,2,0:T(2,128)(2,1)}, u32[]{:S(2)}, u32[]{:S(2)}) async-start(bf16[4,2,1,128,4608]{3,1,4,2,0:T(2,128)(2,1)} %copy.36), calls=%async_computation | async-start | bytes 18874368 | tf_op jit(solution)/shard_map/all_to_all | solution.py:42
  236.2 0.2 fusion.9
  236.4 0.1 multiply_cosine_fusion
  236.6 4.9 %copy.41 = bf16[4,2,1,64,4608]{4,3,0,1,2:T(8,128)(2,1)} copy(bf16[4,2,1,64,4608]{4,3,1,2,0:T(8,128)(2,1)} %all-to-all-done.2) | data formatting | bytes 9437184 | tf_op jit(solution)/shard_map/all_to_all | solution.py:44
  241.4 4.9 %copy.39 = bf16[4,2,1,64,4608]{4,3,0,1,2:T(8,128)(2,1)} copy(bf16[4,2,1,64,4608]{4,3,1,2,0:T(8,128)(2,1)} %all-to-all-done.1) | data formatting | bytes 9437184 | tf_op jit(solution)/shard_map/all_to_all | solution.py:43
  246.3 50.7 %all-gather.8.cloned.1.call-done = bf16[4608,1,1024]{2,0,1:T(8,128)(2,1)} async-done(((bf16[576,1,1024]{2,0,1:T(8,128)(2,1)}), bf16[4608,1,1024]{2,0,1:T(8,128)(2,1)}) %all-gather.8.cloned.1.call-update) | async-done | bytes 9437200 | tf_op jit(solution)/shard_map/all_gather | solution.py:50
  297.0 12.6 %copy.44 = bf16[1024,4608]{1,0:T(8,128)(2,1)} copy(bf16[1024,4608]{0,1:T(8,128)(2,1)} %bitcast.52) | data formatting | bytes 18874368
  309.6 30.8 %all-to-all-done = bf16[4,2,1,128,4608]{3,1,4,2,0:T(2,128)(2,1)} async-done(((bf16[4,2,1,128,4608]{3,1,4,2,0:T(2,128)(2,1)}), bf16[4,2,1,128,4608]{3,1,4,2,0:T(2,128)(2,1)}, u32[]{:S(2)}, u32[]{:S(2)}) %all-to-all-start) | async-done | bytes 9437216 | tf_op jit(solution)/shard_map/all_to_all | solution.py:42
  340.5 23.5 %copy.37 = bf16[4,2,1,128,4608]{4,3,0,1,2:T(8,128)(2,1)} copy(bf16[4,2,1,128,4608]{3,1,4,2,0:T(2,128)(2,1)} %all-to-all-done) | data formatting | bytes 18874368 | tf_op jit(solution)/shard_map/all_to_all | solution.py:42
  363.9 9.2 %fusion.2 = f32[4,2048]{1,0:T(4,128)S(1)} fusion(bf16[512,4608]{1,0:T(8,128)(2,1)} %bitcast.55, bf16[512,4608]{1,0:T(8,128)(2,1)} %bitcast.57, bf16[1024,4608]{1,0:T(8,128)(2,1)} %bitcast.53, bf16[4,4608]{1,0:T(4,128)(2,1)S(1)} %copy-done, f32[4608]{0:T(1024)S(1)} %copy-done.3, f32[4]{0:T(128)S(1)} %add_rsqrt_fusion.1), kind=kOutput, calls=%fused_computation.3 | convolution fusion | flops 132194304 | bytes 18962448 | tf_op jit(solution)/shard_map/dot_general | solution.py:58
  373.2 0.1 subtract_convert_fusion.1
  373.4 0.1 maximum_bitcast_fusion
  373.4 0.2 fusion.16
  373.6 3.5 fusion.22
  377.2 2.9 fusion.8
  380.1 6.9 %fusion = f32[4,4608]{1,0:T(4,128)} fusion(bf16[4,1024]{1,0:T(4,128)(2,1)S(1)} %convert_element_type.56, bf16[4608,1,1024]{2,0,1:T(8,128)(2,1)} %all-gather.8.cloned.1.call-done), kind=kOutput, calls=%fused_computation.1 | convolution fusion | flops 37748736 | bytes 9519104 | tf_op jit(solution)/shard_map/dot_general | solution.py:93
  387.0 16.4 %fusion.3 = bf16[4608,2048]{0,1:T(8,128)(2,1)} fusion(bf16[512,4608]{1,0:T(8,128)(2,1)} %bitcast.56, bf16[512,4608]{1,0:T(8,128)(2,1)} %bitcast.58, bf16[1024,4608]{1,0:T(8,128)(2,1)} %bitcast.54), kind=kLoop, calls=%fused_computation.4 | loop fusion | flops 56623104 | bytes 37748736 | tf_op jit(solution)/shard_map/transpose | solution.py:47
  403.4 24.6 %copy.43 = bf16[4608,2048]{1,0:T(8,128)(2,1)} copy(bf16[4608,2048]{0,1:T(8,128)(2,1)} %fusion.3) | data formatting | bytes 37748736
  428.0 1.0 multiply_reduce_fusion
  429.1 1.4 multiply_convert_fusion
  (31 shorter events, 0.5 us)
Async XLA Ops:
  7.2 56.4 %all-gather.14.cloned.1.call-start = ((), (), s32[]{:S(2)}) async-start(), calls=%async_computation.8 | async-start | bytes 5308416 | tf_op jit(solution)/shard_map/all_gather | solution.py:38
  7.9 107.3 %all-gather.12.cloned.1.call-start = ((), (), s32[]{:S(2)}) async-start(), calls=%async_computation.7 | async-start | bytes 5308416 | tf_op jit(solution)/shard_map/all_gather | solution.py:37
  8.6 197.7 %all-gather.10.cloned.1.call-start = ((), (), s32[]{:S(2)}) async-start(), calls=%async_computation.6 | async-start | bytes 10616832 | tf_op jit(solution)/shard_map/all_gather | solution.py:36
  9.4 287.6 %all-gather.8.cloned.1.call-start = ((), (), s32[]{:S(2)}) async-start(), calls=%async_computation.4 | async-start | bytes 10616832 | tf_op jit(solution)/shard_map/all_gather | solution.py:50
  63.6 58.7 %all-to-all-start.2 = ((bf16[4,2,1,64,4608]{4,3,1,2,0:T(8,128)(2,1)}), bf16[4,2,1,64,4608]{4,3,1,2,0:T(8,128)(2,1)}, u32[]{:S(2)}, u32[]{:S(2)}) async-start(bf16[4,2,1,64,4608]{4,3,1,2,0:T(8,128)(2,1)} %bitcast.61), calls=%async_computation.2 | async-start | bytes 9437184 | tf_op jit(solution)/shard_map/all_to_all | solution.py:44
  122.2 107.9 %all-to-all-start.1 = ((bf16[4,2,1,64,4608]{4,3,1,2,0:T(8,128)(2,1)}), bf16[4,2,1,64,4608]{4,3,1,2,0:T(8,128)(2,1)}, u32[]{:S(2)}, u32[]{:S(2)}) async-start(bf16[4,2,1,64,4608]{4,3,1,2,0:T(8,128)(2,1)} %bitcast.60), calls=%async_computation.1 | async-start | bytes 9437184 | tf_op jit(solution)/shard_map/all_to_all | solution.py:43
  230.1 6.0 %copy-start.2 = (s32[4]{0:T(128)S(1)}, s32[4]{0:T(128)}, u32[]{:S(2)}) copy-start(s32[4]{0:T(128)} %param.11) | copy-start | bytes 52
  230.1 6.1 %copy-start = (bf16[4,4608]{1,0:T(4,128)(2,1)S(1)}, bf16[4,4608]{1,0:T(4,128)(2,1)}, u32[]{:S(2)}) copy-start(bf16[4,4608]{1,0:T(4,128)(2,1)} %param.10) | copy-start | bytes 110596
  230.1 110.3 %all-to-all-start = ((bf16[4,2,1,128,4608]{3,1,4,2,0:T(2,128)(2,1)}), bf16[4,2,1,128,4608]{3,1,4,2,0:T(2,128)(2,1)}, u32[]{:S(2)}, u32[]{:S(2)}) async-start(bf16[4,2,1,128,4608]{3,1,4,2,0:T(2,128)(2,1)} %copy.36), calls=%async_computation | async-start | bytes 18874368 | tf_op jit(solution)/shard_map/all_to_all | solution.py:42
  236.1 191.9 %all-reduce.2.cloned.1.call-start = ((), (), s32[]{:S(2)}) async-start(), calls=%async_computation.5 | async-start | bytes 147456 | tf_op jit(solution)/shard_map/psum | solution.py:95
  309.6 54.3 %copy-start.3 = (f32[4608]{0:T(1024)S(1)}, f32[4608]{0:T(1024)}, u32[]{:S(2)}) copy-start(f32[4608]{0:T(1024)} %param.14) | copy-start | bytes 55300
  403.4 25.7 %copy-start.1 = (f32[1152]{0:T(1024)S(1)}, f32[1152]{0:T(1024)}, u32[]{:S(2)}) copy-start(f32[1152]{0:T(1024)} %param.19) | copy-start | bytes 13828
Sparse Core Ops, SparseCore 0:
  9.6 53.9 all-gather.13
  65.2 49.9 all-gather.11
  116.9 89.4 all-gather.9
  207.9 89.1 all-gather.7
  387.1 38.0 all-reduce.1
where the time goes:
time: 440 us; the launch traced here: 437 us
  waiting for transfers between devices  249 us (57%)
  local copies, waits for them, and re-layouts  95.6 us (22%)
  matrix products  22.7 us (5%)
  blocking collectives  20.6 us (5%)
  other arithmetic  19.4 us (4%)
  starting transfers between devices  16.1 us (4%)
  between operations  13.9 us (3%)
    all_gather x1, waiting for transfers between devices, body(): lax.all_gather(q_proj[None], 'rep', axis=0, tiled=True)  79.1 us
    all_gather x1, waiting for transfers between devices, body(): complete_rows = lax.all_gather(rows_of_group, 'rep', axis=0, tiled=True)  50.7 us
    all_gather x1, waiting for transfers between devices, body(): lax.all_gather(k_proj[None], 'rep', axis=0, tiled=True)  46.7 us
    unnamed x12, local copies, waits for them, and re-layouts  37.2 us
    all_gather x1, waiting for transfers between devices, body(): lax.all_gather(v_proj[None], 'rep', axis=0, tiled=True)  32.1 us
    all_to_all x1, waiting for transfers between devices, body(): lax.all_to_all(shaped[0], 'tp', split_axis=0, concat_axis=2, tiled=True)  30.8 us
    reshape x1, local copies, waits for them, and re-layouts, body(): matrix.reshape((tp_count, per_tp, 1) + matrix.shape[1:])  23.7 us
    all_to_all x1, local copies, waits for them, and re-layouts, body(): lax.all_to_all(shaped[0], 'tp', split_axis=0, concat_axis=2, tiled=True)  23.5 us
  transfers between devices with their start and end apart: 8, of which 6 were waited for; matrix products, arithmetic and copies ran while one was open for 20% of the time, Pallas kernels for 0%

commit v1 on v0

--- a/solution.py
+++ b/solution.py
@@ -5,6 +5,15 @@
 
 score_scale = 144.0 ** (-0.5)
 soft_cap = 50.0
+pair_marks_on_mesh = lambda frame_in, along_dim, array_axis: jnp.concatenate(
+    lax.all_to_all(
+        jnp.stack(jnp.split(frame_in, lax.axis_size("tp"), along_dim), 0),
+        "tp",
+        concat_axis=0,
+        split_axis=0,
+    ),
+    array_axis,
+)
 
 
 def rms_scale(values, gain):
@@ -39,7 +48,7 @@
     )
     shaped = [matrix.reshape((tp_count, per_tp, 1) + matrix.shape[1:]) for matrix in stacked]
     arrived = (
-        lax.all_to_all(shaped[0], "tp", split_axis=0, concat_axis=2, tiled=True),
+        pair_marks_on_mesh(shaped[0], 0, 2),
         lax.all_to_all(shaped[1], "tp", split_axis=0, concat_axis=2, tiled=True),
         lax.all_to_all(shaped[2], "tp", split_axis=0, concat_axis=2, tiled=True),
     )

time: 440 us -> 473 us (1.075)
  other arithmetic: 19.4 us -> 39 us
  local copies, waits for them, and re-layouts: 95.6 us -> 105 us
    all_gather x1, waiting for transfers between devices: 50.7 us -> 16.2 us  [body(): complete_rows = lax.all_gather(rows_of_group, 'rep', axis=0, tiled=True)]
    all_to_all x1, waiting for transfers between devices: 30.8 us -> 64.3 us  [lax.all_to_all(jnp.stack(jnp.split(frame_in, lax.axis_size('tp'), along_d...]
    all_to_all x1, waiting for transfers between devices: 7.02 us -> 34.1 us  [body(): lax.all_to_all(shaped[2], 'tp', split_axis=0, concat_axis=2, tiled=True)]
    another operation x0 -> x4, local copies, waits for them, and re-layouts: none -> 26.1 us  [jnp.stack(jnp.split(frame_in, lax.axis_size('tp'), along_dim), 0)]
    reshape x1 -> x0, local copies, waits for them, and re-layouts: 23.7 us -> none  [body(): matrix.reshape((tp_count, per_tp, 1) + matrix.shape[1:])]
    another operation x2 -> x3, other arithmetic: 0.16 us -> 19.7 us  [the longest x1 19.6 us: jnp.stack(jnp.split(frame_in, lax.axis_size('tp'), along_dim), 0)]
    all_gather x1, waiting for transfers between devices: 46.7 us -> 32.1 us  [body(): lax.all_gather(k_proj[None], 'rep', axis=0, tiled=True)]
    all_gather x1, waiting for transfers between devices: 32.1 us -> 18.4 us  [body(): lax.all_gather(v_proj[None], 'rep', axis=0, tiled=True)]
  transfers between devices with their start and end apart: 8 -> 8, of which waited for: 6 -> 6; matrix products, arithmetic and copies ran while one was open for 20% -> 25% of each run, Pallas kernels for 0% -> 0%
where the time goes in v1:
time: 473 us; the launch traced here: 470 us
  waiting for transfers between devices  253 us (53%)
  local copies, waits for them, and re-layouts  105 us (22%)
  other arithmetic  39 us (8%)
  matrix products  22.7 us (5%)
  blocking collectives  20.6 us (4%)
  starting transfers between devices  15.9 us (3%)
  between operations  13.9 us (3%)
    all_gather x1, waiting for transfers between devices, body(): lax.all_gather(q_proj[None], 'rep', axis=0, tiled=True)  86.2 us
    all_to_all x1, waiting for transfers between devices, lax.all_to_all(jnp.stack(jnp.split(frame_in, lax.axis_size('tp'), along_d...  64.3 us
    unnamed x12, local copies, waits for them, and re-layouts  37.3 us
    all_to_all x1, waiting for transfers between devices, body(): lax.all_to_all(shaped[2], 'tp', split_axis=0, concat_axis=2, tiled=True)  34.1 us
    all_gather x1, waiting for transfers between devices, body(): lax.all_gather(k_proj[None], 'rep', axis=0, tiled=True)  32.1 us
    another operation x4, local copies, waits for them, and re-layouts, jnp.stack(jnp.split(frame_in, lax.axis_size('tp'), along_dim), 0)  26.1 us
    all_to_all x1, local copies, waits for them, and re-layouts, lax.all_to_all(jnp.stack(jnp.split(frame_in, lax.axis_size('tp'), along_d...  23.5 us
    all_to_all x1, blocking collectives, body(): lax.all_to_all(split_cols, 'tp', split_axis=1, concat_axis=0, tiled=True)  20.6 us
  transfers between devices with their start and end apart: 8, of which 6 were waited for; matrix products, arithmetic and copies ran while one was open for 25% of the time, Pallas kernels for 0%

profile of v1, /device:TPU:0, one launch (start us, length us, event | category | flops | bytes accessed | tf_op | source)
XLA Modules:
  0.0 470.5 jit_solution(965838015428295386)
XLA Ops:
  7.2 0.7 all-gather.12.cloned.1.call-update
  7.9 0.7 all-gather.10.cloned.1.call-update
  8.7 0.7 all-gather.14.cloned.1.call-update
  9.4 1.4 copy.73
  10.8 20.6 %all_to_all.53 = bf16[144,4,1024]{2,0,1:T(8,128)(2,1)} all-to-all(bf16[144,4,1024]{2,0,1:T(8,128)(2,1)S(1)} %bitcast.67), channel_id=1, replica_groups=mesh['rep'=8,'tp'=4] {'tp'}, dimensions={1} | all-to-all | bytes 2359296 | tf_op jit(solution)/shard_map/all_to_all | solution.py:58
  31.5 32.1 %all-gather.12.cloned.1.call-done = bf16[512,4608]{1,0:T(8,128)(2,1)} async-done(((bf16[64,4608]{1,0:T(8,128)(2,1)}), bf16[512,4608]{1,0:T(8,128)(2,1)}) %all-gather.12.cloned.1.call-update) | async-done | bytes 4718608 | tf_op jit(solution)/shard_map/all_gather | solution.py:46
  63.6 5.0 %all-to-all-start.1 = ((bf16[4,2,1,64,4608]{4,3,1,2,0:T(8,128)(2,1)}), bf16[4,2,1,64,4608]{4,3,1,2,0:T(8,128)(2,1)}, u32[]{:S(2)}, u32[]{:S(2)}) async-start(bf16[4,2,1,64,4608]{4,3,1,2,0:T(8,128)(2,1)} %bitcast.64), calls=%async_computation.1 | async-start | bytes 9437184 | tf_op jit(solution)/shard_map/all_to_all | solution.py:52
  68.6 86.2 %all-gather.10.cloned.1.call-done = bf16[1024,4608]{1,0:T(8,128)(2,1)} async-done(((bf16[128,4608]{1,0:T(8,128)(2,1)}), bf16[1024,4608]{1,0:T(8,128)(2,1)}) %all-gather.10.cloned.1.call-update) | async-done | bytes 9437200 | tf_op jit(solution)/shard_map/all_gather | solution.py:45
  154.7 6.9 %fusion.22 = (bf16[256,4608]{1,0:T(8,128)(2,1)}, bf16[256,4608]{1,0:T(8,128)(2,1)}, bf16[256,4608]{1,0:T(8,128)(2,1)}, bf16[256,4608]{1,0:T(8,128)(2,1)}) fusion(bf16[1024,4608]{1,0:T(8,128)(2,1)} %all-gather.10.cloned.1.call-done), kind=kLoop, calls=%fused_computation.48 | loop fusion | bytes 18874368 | tf_op jit(solution)/shard_map/split | solution.py:10
  161.6 5.7 %copy.63 = bf16[1,1,2,1,128,4608]{4,2,5,3,1,0:T(2,128)(2,1)S(1)} copy(bf16[1,1,2,1,128,4608]{5,4,2,3,1,0:T(8,128)(2,1)} %bitcast.63) | data formatting | bytes 4718592 | tf_op jit(solution)/shard_map/stack | solution.py:10
  167.3 6.8 %copy.64 = bf16[1,1,2,1,128,4608]{4,2,5,3,1,0:T(2,128)(2,1)} copy(bf16[1,1,2,1,128,4608]{5,4,2,3,1,0:T(8,128)(2,1)} %bitcast.62) | data formatting | bytes 4718592 | tf_op jit(solution)/shard_map/stack | solution.py:10
  174.1 6.8 %copy.65 = bf16[1,1,2,1,128,4608]{4,2,5,3,1,0:T(2,128)(2,1)} copy(bf16[1,1,2,1,128,4608]{5,4,2,3,1,0:T(8,128)(2,1)} %bitcast.61) | data formatting | bytes 4718592 | tf_op jit(solution)/shard_map/stack | solution.py:10
  180.9 6.8 %copy.66 = bf16[1,1,2,1,128,4608]{4,2,5,3,1,0:T(2,128)(2,1)} copy(bf16[1,1,2,1,128,4608]{5,4,2,3,1,0:T(8,128)(2,1)} %bitcast.60) | data formatting | bytes 4718592 | tf_op jit(solution)/shard_map/stack | solution.py:10
  187.7 18.4 %all-gather.14.cloned.1.call-done = bf16[512,4608]{1,0:T(8,128)(2,1)} async-done(((bf16[64,4608]{1,0:T(8,128)(2,1)}), bf16[512,4608]{1,0:T(8,128)(2,1)}) %all-gather.14.cloned.1.call-update) | async-done | bytes 4718608 | tf_op jit(solution)/shard_map/all_gather | solution.py:47
  206.0 5.0 %all-to-all-start.2 = ((bf16[4,2,1,64,4608]{4,3,1,2,0:T(8,128)(2,1)}), bf16[4,2,1,64,4608]{4,3,1,2,0:T(8,128)(2,1)}, u32[]{:S(2)}, u32[]{:S(2)}) async-start(bf16[4,2,1,64,4608]{4,3,1,2,0:T(8,128)(2,1)} %bitcast.65), calls=%async_computation.2 | async-start | bytes 9437184 | tf_op jit(solution)/shard_map/all_to_all | solution.py:53
  211.0 19.6 %pad_maximum_fusion.1 = bf16[4,1,2,1,128,4608]{4,2,5,3,1,0:T(2,128)(2,1)} fusion(bf16[1,1,2,1,128,4608]{4,2,5,3,1,0:T(2,128)(2,1)} %copy.66, bf16[1,1,2,1,128,4608]{4,2,5,3,1,0:T(2,128)(2,1)} %copy.65, bf16[1,1,2,1,128,4608]{4,2,5,3,1,0:T(2,128)(2,1)} %copy.64, bf16[1,1,2,1,128,4608]{4,2,5,3,1,0:T(2,128)(2,1)S(1)} %copy.63), kind=kLoop, calls=%fused_computation.1 | loop fusion | flops 14155776 | bytes 18874368 | tf_op jit(solution)/shard_map/stack | solution.py:10
  230.6 34.1 %all-to-all-done.2 = bf16[4,2,1,64,4608]{4,3,1,2,0:T(8,128)(2,1)} async-done(((bf16[4,2,1,64,4608]{4,3,1,2,0:T(8,128)(2,1)}), bf16[4,2,1,64,4608]{4,3,1,2,0:T(8,128)(2,1)}, u32[]{:S(2)}, u32[]{:S(2)}) %all-to-all-start.2) | async-done | bytes 4718624 | tf_op jit(solution)/shard_map/all_to_all | solution.py:53
  264.7 5.8 %all-to-all-start = ((bf16[4,1,2,1,128,4608]{4,2,5,3,1,0:T(2,128)(2,1)}), bf16[4,1,2,1,128,4608]{4,2,5,3,1,0:T(2,128)(2,1)}, u32[]{:S(2)}, u32[]{:S(2)}) async-start(bf16[4,1,2,1,128,4608]{4,2,5,3,1,0:T(2,128)(2,1)} %pad_maximum_fusion.1), calls=%async_computation | async-start | bytes 18874368 | tf_op jit(solution)/shard_map/all_to_all | solution.py:9
  271.0 5.0 %copy.55 = bf16[4,2,1,64,4608]{4,3,0,1,2:T(8,128)(2,1)} copy(bf16[4,2,1,64,4608]{4,3,1,2,0:T(8,128)(2,1)} %all-to-all-done.1) | data formatting | bytes 9437184 | tf_op jit(solution)/shard_map/all_to_all | solution.py:52
  276.0 4.9 %copy.57 = bf16[4,2,1,64,4608]{4,3,0,1,2:T(8,128)(2,1)} copy(bf16[4,2,1,64,4608]{4,3,1,2,0:T(8,128)(2,1)} %all-to-all-done.2) | data formatting | bytes 9437184 | tf_op jit(solution)/shard_map/all_to_all | solution.py:53
  280.8 16.2 %all-gather.8.cloned.1.call-done = bf16[4608,1,1024]{2,0,1:T(8,128)(2,1)} async-done(((bf16[576,1,1024]{2,0,1:T(8,128)(2,1)}), bf16[4608,1,1024]{2,0,1:T(8,128)(2,1)}) %all-gather.8.cloned.1.call-update) | async-done | bytes 9437200 | tf_op jit(solution)/shard_map/all_gather | solution.py:59
  297.0 12.6 %copy.60 = bf16[1024,4608]{1,0:T(8,128)(2,1)} copy(bf16[1024,4608]{0,1:T(8,128)(2,1)} %bitcast.53) | data formatting | bytes 18874368
  309.6 64.3 %all-to-all-done = bf16[4,1,2,1,128,4608]{4,2,5,3,1,0:T(2,128)(2,1)} async-done(((bf16[4,1,2,1,128,4608]{4,2,5,3,1,0:T(2,128)(2,1)}), bf16[4,1,2,1,128,4608]{4,2,5,3,1,0:T(2,128)(2,1)}, u32[]{:S(2)}, u32[]{:S(2)}) %all-to-all-start) | async-done | bytes 9437216 | tf_op jit(solution)/shard_map/all_to_all | solution.py:9
  373.9 23.5 %copy.53 = bf16[4,1,2,1,128,4608]{5,4,0,2,3,1:T(8,128)(2,1)} copy(bf16[4,1,2,1,128,4608]{4,2,5,3,1,0:T(2,128)(2,1)} %all-to-all-done) | data formatting | bytes 18874368 | tf_op jit(solution)/shard_map/all_to_all | solution.py:9
  397.4 9.2 %fusion.2 = f32[4,2048]{1,0:T(4,128)S(1)} fusion(bf16[512,4608]{1,0:T(8,128)(2,1)} %bitcast.58, bf16[512,4608]{1,0:T(8,128)(2,1)} %bitcast.56, bf16[1024,4608]{1,0:T(8,128)(2,1)} %bitcast.54, bf16[4,4608]{1,0:T(4,128)(2,1)S(1)} %copy-done, f32[4608]{0:T(1024)S(1)} %copy-done.3, f32[4]{0:T(128)S(1)} %add_rsqrt_fusion.1), kind=kOutput, calls=%fused_computation.4 | convolution fusion | flops 132194304 | bytes 18962448 | tf_op jit(solution)/shard_map/dot_general | solution.py:67
  407.1 3.5 fusion.23
  410.7 2.9 fusion.8
  413.6 6.9 %fusion = f32[4,4608]{1,0:T(4,128)} fusion(bf16[4,1024]{1,0:T(4,128)(2,1)S(1)} %convert_element_type.56, bf16[4608,1,1024]{2,0,1:T(8,128)(2,1)} %all-gather.8.cloned.1.call-done), kind=kOutput, calls=%fused_computation.2 | convolution fusion | flops 37748736 | bytes 9519104 | tf_op jit(solution)/shard_map/dot_general | solution.py:102
  420.5 16.4 %fusion.3 = bf16[4608,2048]{0,1:T(8,128)(2,1)} fusion(bf16[512,4608]{1,0:T(8,128)(2,1)} %bitcast.59, bf16[512,4608]{1,0:T(8,128)(2,1)} %bitcast.57, bf16[1024,4608]{1,0:T(8,128)(2,1)} %bitcast.55), kind=kLoop, calls=%fused_computation.5 | loop fusion | flops 56623104 | bytes 37748736 | tf_op jit(solution)/shard_map/transpose | solution.py:56
  436.9 24.6 %copy.59 = bf16[4608,2048]{1,0:T(8,128)(2,1)} copy(bf16[4608,2048]{0,1:T(8,128)(2,1)} %fusion.3) | data formatting | bytes 37748736
  461.5 1.0 multiply_reduce_fusion
  462.6 1.4 multiply_convert_fusion
  (36 shorter events, 1.1 us)
Async XLA Ops:
  7.2 56.4 %all-gather.12.cloned.1.call-start = ((), (), s32[]{:S(2)}) async-start(), calls=%async_computation.7 | async-start | bytes 5308416 | tf_op jit(solution)/shard_map/all_gather | solution.py:46
  7.9 146.8 %all-gather.10.cloned.1.call-start = ((), (), s32[]{:S(2)}) async-start(), calls=%async_computation.6 | async-start | bytes 10616832 | tf_op jit(solution)/shard_map/all_gather | solution.py:45
  8.6 197.4 %all-gather.14.cloned.1.call-start = ((), (), s32[]{:S(2)}) async-start(), calls=%async_computation.8 | async-start | bytes 5308416 | tf_op jit(solution)/shard_map/all_gather | solution.py:47
  9.4 287.6 %all-gather.8.cloned.1.call-start = ((), (), s32[]{:S(2)}) async-start(), calls=%async_computation.4 | async-start | bytes 10616832 | tf_op jit(solution)/shard_map/all_gather | solution.py:59
  63.6 142.4 %all-to-all-start.1 = ((bf16[4,2,1,64,4608]{4,3,1,2,0:T(8,128)(2,1)}), bf16[4,2,1,64,4608]{4,3,1,2,0:T(8,128)(2,1)}, u32[]{:S(2)}, u32[]{:S(2)}) async-start(bf16[4,2,1,64,4608]{4,3,1,2,0:T(8,128)(2,1)} %bitcast.64), calls=%async_computation.1 | async-start | bytes 9437184 | tf_op jit(solution)/shard_map/all_to_all | solution.py:52
  206.0 58.7 %all-to-all-start.2 = ((bf16[4,2,1,64,4608]{4,3,1,2,0:T(8,128)(2,1)}), bf16[4,2,1,64,4608]{4,3,1,2,0:T(8,128)(2,1)}, u32[]{:S(2)}, u32[]{:S(2)}) async-start(bf16[4,2,1,64,4608]{4,3,1,2,0:T(8,128)(2,1)} %bitcast.65), calls=%async_computation.2 | async-start | bytes 9437184 | tf_op jit(solution)/shard_map/all_to_all | solution.py:53
  230.6 40.0 %copy-start.2 = (s32[4]{0:T(128)S(1)}, s32[4]{0:T(128)}, u32[]{:S(2)}) copy-start(s32[4]{0:T(128)} %param.11) | copy-start | bytes 52
  230.6 40.0 %copy-start = (bf16[4,4608]{1,0:T(4,128)(2,1)S(1)}, bf16[4,4608]{1,0:T(4,128)(2,1)}, u32[]{:S(2)}) copy-start(bf16[4,4608]{1,0:T(4,128)(2,1)} %param.10) | copy-start | bytes 110596
  264.7 109.2 %all-to-all-start = ((bf16[4,1,2,1,128,4608]{4,2,5,3,1,0:T(2,128)(2,1)}), bf16[4,1,2,1,128,4608]{4,2,5,3,1,0:T(2,128)(2,1)}, u32[]{:S(2)}, u32[]{:S(2)}) async-start(bf16[4,1,2,1,128,4608]{4,2,5,3,1,0:T(2,128)(2,1)} %pad_maximum_fusion.1), calls=%async_computation | async-start | bytes 18874368 | tf_op jit(solution)/shard_map/all_to_all | solution.py:9
  270.5 191.0 %all-reduce.2.cloned.1.call-start = ((), (), s32[]{:S(2)}) async-start(), calls=%async_computation.5 | async-start | bytes 147456 | tf_op jit(solution)/shard_map/psum | solution.py:104
  309.6 87.8 %copy-start.3 = (f32[4608]{0:T(1024)S(1)}, f32[4608]{0:T(1024)}, u32[]{:S(2)}) copy-start(f32[4608]{0:T(1024)} %param.14) | copy-start | bytes 55300
  436.9 25.7 %copy-start.1 = (f32[1152]{0:T(1024)S(1)}, f32[1152]{0:T(1024)}, u32[]{:S(2)}) copy-start(f32[1152]{0:T(1024)} %param.19) | copy-start | bytes 13828
Sparse Core Ops, SparseCore 0:
  9.6 53.9 all-gather.11
  65.2 89.4 all-gather.9
  156.4 49.6 all-gather.13
  207.5 89.4 all-gather.7
  420.6 38.7 all-reduce.1
